TPU v7x, 32 devices: a whole 2x2x4 slice. The times are simulated.
32 devices in a mesh: row: 8 (over z, y), expert: 4 (over x, core).
Axes of the slice: x: 2, y: 2, z: 4, core: 2. Of those that a mesh axis runs over, the one named last changes fastest.
Arguments:
- base: bfloat16 [8, 7168, 2048], P('expert', 'row'), may hold values from -6 to 6
- left_factors: bfloat16 [8, 7168, 64], P('expert', None, 'row'), may hold values from -6 to 6
- right_factors: bfloat16 [8, 64, 2048], P('expert', None, 'row'), may hold values from -0.75 to 0.75
- expert_adapter_scale: float32 [8], P('expert'), may hold values from 0.5 to 2
- placement: int32 [8], P('expert'), may hold values from 0 to 3, as said below
Outputs:
- serving: bfloat16 [8, 7168, 2048], P('expert', None, 'row')
Inputs may be any that keep to these rules, and one draw needn't show every extreme that they name: `placement`: expert g * 2 + j is placed on (g + o_j) mod (4) for one offset o_j per slot j, the same for every g; the offsets of slots 0 and 1 add up to 3.
All inputs are finite; a program needn't handle non-finite values.
Results may differ from a plain program's by a relative error of at most 0.001.
Values may be sent and summed in bfloat16 or wider, within the bound.
A program may use at most 64 MiB of HBM per device.

v0:
```python
import functools

import jax
import jax.numpy as jnp
from jax import lax
from jax.experimental import pallas as pl
from jax.experimental.pallas import tpu as pltpu
from jax.sharding import PartitionSpec as P

MESH = pl.DeviceIdType.MESH
WINDOW = 8
LANES = 128


def unit_of(height):
    return next(u for u in (1, 2, 4, 8) if u * height % LANES == 0)


def near_turn(q, half):
    quarter = half // 2
    return (q + q // quarter) % half + quarter * (1 - (q + half - 1) // half)


def piece_order(rows, unit):
    half = rows // 2
    order = []
    for q in range(half // unit):
        for m in (half + q * unit, near_turn(q, half // unit) * unit):
            order += range(m, m + unit)
    return order


def exchange_kernel(dist, groups, rows, base, left, right, scale, out, got, left_all, right_got, scale_got,
                    send, recv, lsend, lrecv, ssend, srecv, osem):
    r, g = lax.axis_index("row"), lax.axis_index("expert")
    slots, _, height, width = got.shape
    to = [lax.rem(g + d, groups) for d in dist]

    barrier = pltpu.get_barrier_semaphore()
    steps = sorted({d for d in dist} | {(groups - d) % groups for d in dist} | {0})
    for e in steps:
        for m in range(rows):
            if e == 0 and m == 0:
                continue
            pl.semaphore_signal(barrier, inc=1, device_id={"row": r ^ m, "expert": lax.rem(g + e, groups)},
                                device_id_type=MESH)
    pl.semaphore_wait(barrier, len(steps) * rows - 1)

    def remote(src, dst, s, t, row, expert):
        return pltpu.make_async_remote_copy(src_ref=src, dst_ref=dst, send_sem=s, recv_sem=t,
                                            device_id={"row": row, "expert": expert}, device_id_type=MESH)

    first = []
    for j in range(slots):
        for src, dst, s, t in (
            (left.at[j], left_all.at[j, r], lsend.at[j, 0], lrecv.at[j, 0]),
            (right.at[j], right_got.at[j], ssend.at[j, 0], srecv.at[j, 0]),
            (scale.at[j], scale_got.at[j], ssend.at[j, 1], srecv.at[j, 1]),
        ):
            if dist[j] == 0:
                copy = pltpu.make_async_copy(src, dst, t)
            else:
                copy = remote(src, dst, s, t, r, to[j])
            copy.start()
            first.append(copy)

    def left_round(mask, held):
        copies = []
        for s in held:
            for j in range(slots):
                piece = left_all.at[j, r ^ s]
                copy = remote(piece, piece, lsend.at[j, mask | s], lrecv.at[j, mask | s], r ^ mask, g)
                copy.start()
                copies.append(copy)
        return copies

    rounds = []
    mask, held = rows // 2, [0]
    while mask:
        rounds.append((mask, list(held)))
        held += [s | mask for s in held]
        mask //= 2

    pieces = [(m, j) for m in piece_order(rows, unit_of(height)) for j in range(slots)]
    at = {1 + i * (len(pieces) // len(rounds)): i for i in range(len(rounds))}
    pending, waiting = [], first
    for k, (m, j) in enumerate(pieces):
        if k in at:
            for copy in waiting:
                copy.wait()
            waiting = left_round(*rounds[at[k]])
        if len(pending) >= WINDOW:
            pending.pop(0).wait_send()
        c = r ^ m
        src = base.at[j, :, pl.ds(pl.multiple_of(c * width, width), width)]
        if m == 0 and dist[j] == 0:
            pltpu.make_async_copy(src, got.at[j, r], recv.at[j, 0]).start()
        else:
            copy = remote(src, got.at[j, r], send.at[j, m], recv.at[j, m], c, to[j])
            copy.start()
            pending.append(copy)
    for copy in waiting:
        copy.wait()

    unit = unit_of(height)
    half = rows // 2
    turns = rows * slots // unit

    def place(t):
        q, f, j = t // (2 * slots), t // slots % 2, t % slots
        m = (1 - f) * (half + q * unit) + f * near_turn(q, half // unit) * unit
        return m, j, (r ^ m) // unit * unit

    def written(t):
        m, j, row = place(t)
        rows_of = pl.ds(pl.multiple_of(row, unit), unit)
        return pltpu.make_async_copy(got.at[j, rows_of], out.at[j, rows_of], osem.at[t])

    def turn(t, carry):
        m, j, row = place(t)
        for u in range(unit):
            block = got.at[j, r ^ (m + u)]
            remote(block, block, send.at[j, m + u], recv.at[j, m + u], r ^ 1, g).wait_recv()
        rank_all = left_all.shape[1] * left_all.shape[2]
        columns = pl.ds(pl.multiple_of(row * height, LANES), unit * height)
        a = left_all[j, :, :, columns].reshape(rank_all, unit * height)
        delta = lax.dot_general(a, right_got[j], (((0,), (0,)), ((), ())), preferred_element_type=jnp.float32)
        weight = scale_got[j, 0:1, 0:1]
        for u in range(unit):
            part = delta[u * height:(u + 1) * height]
            got[j, row + u] = (got[j, row + u].astype(jnp.float32) + weight * part).astype(got.dtype)
        written(t).start()
        return carry

    lax.fori_loop(0, turns, turn, 0)
    for copy in pending:
        copy.wait_send()

    def settle(t, carry):
        written(t).wait()
        return carry

    lax.fori_loop(0, turns, settle, 0)


def exchange(first, groups, rows, base, left, right, scale):
    dist = (first, groups - 1 - first)
    slots, height, total = base.shape
    width = total // rows
    rank, model = left.shape[1:]
    anywhere = pl.BlockSpec(memory_space=pl.ANY)
    dma = pltpu.SemaphoreType.DMA
    return pl.pallas_call(
        functools.partial(exchange_kernel, dist, groups, rows),
        out_shape=jax.ShapeDtypeStruct((slots, rows, height, width), base.dtype),
        in_specs=[anywhere] * 4,
        out_specs=anywhere,
        scratch_shapes=[
            pltpu.VMEM((slots, rows, height, width), base.dtype),
            pltpu.VMEM((slots, rows, rank, model), left.dtype),
            pltpu.VMEM(right.shape, right.dtype),
            pltpu.VMEM(scale.shape, scale.dtype),
            dma((slots, rows)), dma((slots, rows)),
            dma((slots, rows)), dma((slots, rows)),
            dma((slots, 2)), dma((slots, 2)),
            dma((slots * rows,)),
        ],
        compiler_params=pltpu.CompilerParams(collective_id=first, has_side_effects=True),
        name=f"exchange_{first}",
    )(base, left, right, scale)


def copy_out_kernel(chunks, x, y, held, rsem, wsem):
    size = x.shape[1] // chunks
    reads, writes = [], []
    for j in range(x.shape[0]):
        for i in range(chunks):
            here = pl.ds(i * size, size)
            reads.append(pltpu.make_async_copy(x.at[j, here], held.at[j, here], rsem.at[j, i]))
            writes.append(pltpu.make_async_copy(held.at[j, here], y.at[j, here], wsem.at[j, i]))
    for copy in reads:
        copy.start()
    for read, write in zip(reads, writes):
        read.wait()
        write.start()
    for copy in writes:
        copy.wait()


def copy_out(x, chunks=7):
    dma = pltpu.SemaphoreType.DMA
    anywhere = pl.BlockSpec(memory_space=pl.ANY)
    return pl.pallas_call(
        functools.partial(copy_out_kernel, chunks),
        out_shape=jax.ShapeDtypeStruct(x.shape, x.dtype),
        in_specs=[anywhere],
        out_specs=anywhere,
        scratch_shapes=[pltpu.VMEM(x.shape, x.dtype), dma((x.shape[0], chunks)), dma((x.shape[0], chunks))],
        name="copy_out",
    )(x)


def local(groups, rows, base, left_factors, right_factors, expert_adapter_scale, placement):
    first = jnp.mod(placement[0] - lax.axis_index("expert"), groups)
    slots = base.shape[0]
    left = jnp.swapaxes(left_factors, 1, 2)
    scale = jnp.broadcast_to(expert_adapter_scale[:, None, None], (slots, 8, 128))
    served = lax.switch(
        first,
        [functools.partial(exchange, o, groups, rows) for o in range(groups)],
        base, left, right_factors, scale,
    )
    return copy_out(served.reshape(slots, left.shape[2], served.shape[3]))


def solution(mesh):
    placed = (
        P("expert", "row", None),
        P("expert", None, "row"),
        P("expert", None, "row"),
        P("expert"),
        P("expert"),
    )
    return jax.shard_map(
        functools.partial(local, mesh.shape["expert"], mesh.shape["row"]),
        mesh=mesh, in_specs=placed, out_specs=P("expert", None, "row"), check_vma=False,
    )
```

profile of v0, /device:TPU:16, one launch (start us, length us, event | category | flops | bytes accessed | tf_op | source)
XLA Modules:
  0.0 183.6 jit_solution(17835697948100511039)
XLA Ops:
  0.7 0.7 broadcast_in_dim.2
  1.4 176.2 %conditional.1 = (bf16[2,8,896,256]{3,2,1,0:T(8,128)(2,1)}) conditional(s32[]{:T(128)} %clamp.3, (bf16[2,896,2048]{2,1,0:T(8,128)(2,1)}, bf16[2,8,7168]{2,1,0:T(8,128)(2,1)}, bf16[2,64,256]{2,1,0:T(8,128)(2,1)}, f32[2,8,128]{2,1,0:T(8,128)S(1)}) %tuple.22, (bf16[2,896,2048]{2,1,0:T(8,128)(2,1)}, ...), branch_computations={%region_0.1_spmd, %region_1.2_spmd, %region_2.3_spmd, %region_3.4_... | conditional | bytes 8 | solution.py:208
  1.4 176.2 %exchange_0.1 = bf16[2,8,896,256]{3,2,1,0:T(8,128)(2,1)} custom-call(bf16[2,896,2048]{2,1,0:T(8,128)(2,1)} %get-tuple-element.40.base, bf16[2,8,7168]{2,1,0:T(8,128)(2,1)} %get-tuple-element.42.left, bf16[2,64,256]{2,1,0:T(8,128)(2,1)} %get-tuple-element.44.right, f32[2,8,128]{2,1,0:T(8,128)S(1)} %get-tuple-element.45.scale), custom_call_target="tpu_custom_call" | custom-call | tf_op jit(solution)/shard_map/cond/branch_0_fun/exchange_0/pallas_call | solution.py:153
  177.6 6.0 %copy_out.1 = bf16[2,7168,256]{2,1,0:T(8,128)(2,1)} custom-call(bf16[2,7168,256]{2,1,0:T(8,128)(2,1)} %bitcast.4), custom_call_target="tpu_custom_call" | custom-call | tf_op jit(solution)/shard_map/copy_out/pallas_call | solution.py:193
where the time goes:
time: 184 us
  Pallas kernels  182 us (99%)
    pallas_call x1, Pallas kernels, exchange(): pl.pallas_call(functools.partial(exchange_kernel, dist, groups, rows), ou...  176 us
    pallas_call x1, Pallas kernels, copy_out(): pl.pallas_call(functools.partial(copy_out_kernel, chunks), out_shape=jax....  5.97 us

commit v1 on v0

--- a/solution.py
+++ b/solution.py
@@ -10,6 +10,7 @@
 MESH = pl.DeviceIdType.MESH
 WINDOW = 8
 LANES = 128
+VMEM_LIMIT = 24 << 20
 
 
 def unit_of(height):
@@ -30,8 +31,8 @@
     return order
 
 
-def exchange_kernel(dist, groups, rows, base, left, right, scale, out, got, left_all, right_got, scale_got,
-                    send, recv, lsend, lrecv, ssend, srecv, osem):
+def exchange_kernel(dist, groups, rows, base, left, right, scale, got, left_all, right_got, scale_got,
+                    send, recv, lsend, lrecv, ssend, srecv):
     r, g = lax.axis_index("row"), lax.axis_index("expert")
     slots, _, height, width = got.shape
     to = [lax.rem(g + d, groups) for d in dist]
@@ -111,11 +112,6 @@
         m = (1 - f) * (half + q * unit) + f * near_turn(q, half // unit) * unit
         return m, j, (r ^ m) // unit * unit
 
-    def written(t):
-        m, j, row = place(t)
-        rows_of = pl.ds(pl.multiple_of(row, unit), unit)
-        return pltpu.make_async_copy(got.at[j, rows_of], out.at[j, rows_of], osem.at[t])
-
     def turn(t, carry):
         m, j, row = place(t)
         for u in range(unit):
@@ -129,18 +125,11 @@
         for u in range(unit):
             part = delta[u * height:(u + 1) * height]
             got[j, row + u] = (got[j, row + u].astype(jnp.float32) + weight * part).astype(got.dtype)
-        written(t).start()
         return carry
 
     lax.fori_loop(0, turns, turn, 0)
     for copy in pending:
         copy.wait_send()
-
-    def settle(t, carry):
-        written(t).wait()
-        return carry
-
-    lax.fori_loop(0, turns, settle, 0)
 
 
 def exchange(first, groups, rows, base, left, right, scale):
@@ -150,52 +139,46 @@
     rank, model = left.shape[1:]
     anywhere = pl.BlockSpec(memory_space=pl.ANY)
     dma = pltpu.SemaphoreType.DMA
-    return pl.pallas_call(
+    served = pl.pallas_call(
         functools.partial(exchange_kernel, dist, groups, rows),
         out_shape=jax.ShapeDtypeStruct((slots, rows, height, width), base.dtype),
         in_specs=[anywhere] * 4,
-        out_specs=anywhere,
+        out_specs=pl.BlockSpec(memory_space=pltpu.VMEM),
         scratch_shapes=[
-            pltpu.VMEM((slots, rows, height, width), base.dtype),
             pltpu.VMEM((slots, rows, rank, model), left.dtype),
             pltpu.VMEM(right.shape, right.dtype),
             pltpu.VMEM(scale.shape, scale.dtype),
             dma((slots, rows)), dma((slots, rows)),
             dma((slots, rows)), dma((slots, rows)),
             dma((slots, 2)), dma((slots, 2)),
-            dma((slots * rows,)),
         ],
-        compiler_params=pltpu.CompilerParams(collective_id=first, has_side_effects=True),
+        compiler_params=pltpu.CompilerParams(collective_id=first, has_side_effects=True, vmem_limit_bytes=VMEM_LIMIT),
         name=f"exchange_{first}",
     )(base, left, right, scale)
-
-
-def copy_out_kernel(chunks, x, y, held, rsem, wsem):
+    return copy_out(served.reshape(slots, rows * height, width))
+
+
+def copy_out_kernel(chunks, x, y, sem):
     size = x.shape[1] // chunks
-    reads, writes = [], []
+    copies = []
     for j in range(x.shape[0]):
         for i in range(chunks):
             here = pl.ds(i * size, size)
-            reads.append(pltpu.make_async_copy(x.at[j, here], held.at[j, here], rsem.at[j, i]))
-            writes.append(pltpu.make_async_copy(held.at[j, here], y.at[j, here], wsem.at[j, i]))
-    for copy in reads:
+            copies.append(pltpu.make_async_copy(x.at[j, here], y.at[j, here], sem.at[j, i]))
+    for copy in copies:
         copy.start()
-    for read, write in zip(reads, writes):
-        read.wait()
-        write.start()
-    for copy in writes:
+    for copy in copies:
         copy.wait()
 
 
 def copy_out(x, chunks=7):
-    dma = pltpu.SemaphoreType.DMA
-    anywhere = pl.BlockSpec(memory_space=pl.ANY)
     return pl.pallas_call(
         functools.partial(copy_out_kernel, chunks),
-        out_shape=jax.ShapeDtypeStruct(x.shape, x.dtype),
-        in_specs=[anywhere],
-        out_specs=anywhere,
-        scratch_shapes=[pltpu.VMEM(x.shape, x.dtype), dma((x.shape[0], chunks)), dma((x.shape[0], chunks))],
+        out_shape=pltpu.HBM(x.shape, x.dtype),
+        in_specs=[pl.BlockSpec(memory_space=pltpu.VMEM)],
+        out_specs=pl.BlockSpec(memory_space=pl.ANY),
+        scratch_shapes=[pltpu.SemaphoreType.DMA((x.shape[0], chunks))],
+        compiler_params=pltpu.CompilerParams(vmem_limit_bytes=VMEM_LIMIT),
         name="copy_out",
     )(x)
 
@@ -210,7 +193,7 @@
         [functools.partial(exchange, o, groups, rows) for o in range(groups)],
         base, left, right_factors, scale,
     )
-    return copy_out(served.reshape(slots, left.shape[2], served.shape[3]))
+    return served
 
 
 def solution(mesh):

time: 184 us -> 180 us (0.978)
  Pallas kernels: 182 us -> 179 us
    pallas_call x1, Pallas kernels: 5.97 us -> 3.08 us  [copy_out(): pl.pallas_call(functools.partial(copy_out_kernel, chunks), out_shape=pltp...]
where the time goes in v1:
time: 180 us
  Pallas kernels  179 us (99%)
    pallas_call x1, Pallas kernels, exchange(): pl.pallas_call(functools.partial(exchange_kernel, dist, groups, rows), ou...  175 us

profile of v1, /device:TPU:16, one launch (start us, length us, event | category | flops | bytes accessed | tf_op | source)
XLA Modules:
  0.0 180.0 jit_solution(4046747107344156938)
XLA Ops:
  0.7 179.3 %conditional.1 = (bf16[2,7168,256]{2,1,0:T(8,128)(2,1)}) conditional(s32[]{:T(128)} %clamp.3, (bf16[2,896,2048]{2,1,0:T(8,128)(2,1)}, bf16[2,8,7168]{2,1,0:T(8,128)(2,1)}, bf16[2,64,256]{2,1,0:T(8,128)(2,1)}, f32[2]{0:T(128)}) %tuple.26, (bf16[2,896,2048]{2,1,0:T(8,128)(2,1)}, bf16[2,8,7168]{2,1,0:T(8,128)(2,1)}, ...), branch_computations={%region_0.1_spmd, %region_1.2_spmd, %region_2.3_spmd, %region_3.4_... | conditional | bytes 8208 | solution.py:191
  0.7 0.7 broadcast_in_dim.10.scale
  1.4 175.5 %exchange_3.1 = bf16[2,8,896,256]{3,2,1,0:T(8,128)(2,1)S(1)} custom-call(bf16[2,896,2048]{2,1,0:T(8,128)(2,1)} %get-tuple-element.74.base, bf16[2,8,7168]{2,1,0:T(8,128)(2,1)} %get-tuple-element.55.left, bf16[2,64,256]{2,1,0:T(8,128)(2,1)} %get-tuple-element.78.right, f32[2,8,128]{2,1,0:T(8,128)S(1)} %broadcast_in_dim.10.scale), custom_call_target="tpu_custom_call" | custom-call | tf_op jit(solution)/shard_map/cond/branch_3_fun/exchange_3/pallas_call | solution.py:142
  176.9 3.1 %copy_out.7 = bf16[2,7168,256]{2,1,0:T(8,128)(2,1)} custom-call(bf16[2,7168,256]{2,1,0:T(8,128)(2,1)S(1)} %bitcast.10), custom_call_target="tpu_custom_call" | custom-call | tf_op jit(solution)/shard_map/cond/branch_3_fun/copy_out/pallas_call | solution.py:175

commit v2 on v1

v2 whole, which is shorter than its diff:
```python
import functools

import jax
import jax.numpy as jnp
from jax import lax
from jax.experimental import pallas as pl
from jax.experimental.pallas import tpu as pltpu
from jax.sharding import PartitionSpec as P

MESH = pl.DeviceIdType.MESH
WINDOW = 12
LANES = 128
VMEM_LIMIT = 24 << 20


def unit_of(height):
    return next(u for u in (1, 2, 4, 8) if u * height % LANES == 0)


def near_turn(q, half):
    quarter = half // 2
    return (q + q // quarter) % half + quarter * (1 - (q + half - 1) // half)


def piece_order(rows, slots, lead):
    half = rows // 2
    order = []
    for q in range(half):
        for m in (half + q, near_turn(q, half)):
            order += [(m, (lead + i) % slots) for i in range(slots)]
    return order


def exchange_kernel(dist, groups, rows, base, left, right, scale, got, left_all, right_got, scale_got,
                    send, recv, tsend, trecv, lsend, lrecv, ssend, srecv, go):
    r, g = lax.axis_index("row"), lax.axis_index("expert")
    slots, _, height, width = got.shape
    half, quarter = rows // 2, rows // 4
    to = [lax.rem(g + d, groups) for d in dist]
    lead = min(range(slots), key=lambda j: min(dist[j], groups - dist[j]))
    order = piece_order(rows, slots, lead)
    mirror = half + quarter
    inner = jnp.logical_and(r >= quarter, r < rows - quarter)

    barrier = pltpu.get_barrier_semaphore()

    def enter(row, expert):
        pl.semaphore_signal(barrier, inc=1, device_id={"row": row, "expert": expert}, device_id_type=MESH)

    @pl.when(inner)
    def _():
        enter(r ^ mirror, lax.rem(g + groups - dist[lead], groups))

    steps = sorted({d for d in dist} | {(groups - d) % groups for d in dist} | {0})
    for e in steps:
        for row in (*range(quarter), *range(rows - quarter, rows)):
            if e:
                enter(row, lax.rem(g + e, groups))
            else:
                pl.when(r != row)(functools.partial(enter, row, g))
    pl.semaphore_wait(barrier, jnp.where(inner, 1, len(steps) * rows - 1))

    def remote(src, dst, s, t, row, expert):
        return pltpu.make_async_remote_copy(src_ref=src, dst_ref=dst, send_sem=s, recv_sem=t,
                                            device_id={"row": row, "expert": expert}, device_id_type=MESH)

    cuts = [(0, height)]
    if height % LANES == 0 and height > LANES:
        top = (height // LANES + 1) // 2 * LANES
        cuts = [(0, top), (top, height - top)]

    def tail(j, i):
        off, size = cuts[i]
        c = r ^ (rows - 1)
        src = base.at[j, pl.ds(off, size), pl.ds(pl.multiple_of(c * width, width), width)]
        return remote(src, got.at[j, r, pl.ds(off, size)], tsend.at[j, i], trecv.at[j, i], c, to[j])

    def piece(m, j):
        if m == rows - 1 and len(cuts) > 1:
            return [tail(j, i) for i in range(len(cuts))]
        if j == lead and m in (half, mirror):
            m = jnp.where(inner, half + mirror - m, m)
        c = r ^ m
        src = base.at[j, :, pl.ds(pl.multiple_of(c * width, width), width)]
        if dist[j] == 0 and isinstance(m, int) and m == 0:
            return [pltpu.make_async_copy(src, got.at[j, r], recv.at[j, 0])]
        return [remote(src, got.at[j, r], send.at[j, m], recv.at[j, m], c, to[j])]

    pending = piece(*order[0])

    @pl.when(inner)
    def _():
        pending[0].start()
        pl.semaphore_wait(go, 1)

    @pl.when(jnp.logical_not(inner))
    def _():
        pl.semaphore_signal(go, inc=1, device_id={"row": r ^ quarter, "expert": g}, device_id_type=MESH)

    first = []
    for j in range(slots):
        for src, dst, s, t in (
            (left.at[j], left_all.at[j, r], lsend.at[j, 0], lrecv.at[j, 0]),
            (right.at[j], right_got.at[j], ssend.at[j, 0], srecv.at[j, 0]),
            (scale, scale_got.at[j], ssend.at[j, 1], srecv.at[j, 1]),
        ):
            if dist[j] == 0:
                copy = pltpu.make_async_copy(src, dst, t)
            else:
                copy = remote(src, dst, s, t, r, to[j])
            copy.start()
            first.append(copy)
        copy = remote(left.at[j], left_all.at[j, r], lsend.at[j, half], lrecv.at[j, half], r ^ half, to[j])
        copy.start()
        first.append(copy)

    pl.when(jnp.logical_not(inner))(pending[0].start)

    def left_round(mask, held):
        copies = []
        for s in held:
            for j in range(slots):
                part = left_all.at[j, r ^ s]
                copy = remote(part, part, lsend.at[j, mask | s], lrecv.at[j, mask | s], r ^ mask, g)
                copy.start()
                copies.append(copy)
        return copies

    rounds = []
    mask, held = half // 2, [0, half]
    while mask:
        rounds.append((mask, list(held)))
        held += [s | mask for s in held]
        mask //= 2

    at = {(2 + i) * len(order) // 4: i for i in range(len(rounds))}
    waiting = first
    for k, (m, j) in enumerate(order[1:], 1):
        if k in at:
            for copy in waiting:
                copy.wait()
            waiting = left_round(*rounds[at[k]])
        if len(pending) >= WINDOW:
            pending.pop(0).wait_send()
        copies = piece(m, j)
        for copy in copies:
            copy.start()
        if not (m == 0 and dist[j] == 0):
            pending += copies
    for copy in waiting:
        copy.wait()

    unit = unit_of(height)
    rank_all = left_all.shape[1] * left_all.shape[2]

    def merge(j, row, off, size):
        columns = pl.ds(pl.multiple_of(row * height + off, LANES), size)
        a = left_all[j, :, :, columns].reshape(rank_all, size)
        return lax.dot_general(a, right_got[j], (((0,), (0,)), ((), ())), preferred_element_type=jnp.float32)

    def turn(t, carry):
        m, j = t // slots * unit, t % slots
        row = (r ^ m) // unit * unit
        for u in range(unit):
            block = got.at[j, r ^ (m + u)]
            remote(block, block, send.at[j, m + u], recv.at[j, m + u], r ^ 1, g).wait_recv()
        delta = merge(j, row, 0, unit * height)
        for u in range(unit):
            part = delta[u * height:(u + 1) * height]
            got[j, row + u] = (got[j, row + u].astype(jnp.float32) + scale_got[j, j] * part).astype(got.dtype)
        return carry

    last = 1 if len(cuts) > 1 else 0
    lax.fori_loop(0, rows * slots // unit - last * slots, turn, 0)

    row = r ^ (rows - 1)
    for j in range(slots if last else 0):
        for i, (off, size) in enumerate(cuts):
            tail(j, i).wait_recv()
            here = pl.ds(off, size)
            part = scale_got[j, j] * merge(j, row, off, size)
            got[j, row, here] = (got[j, row, here].astype(jnp.float32) + part).astype(got.dtype)
    for copy in pending:
        copy.wait_send()


def exchange(first, groups, rows, base, left, right, scale):
    dist = (first, groups - 1 - first)
    slots, height, total = base.shape
    width = total // rows
    rank, model = left.shape[1:]
    anywhere = pl.BlockSpec(memory_space=pl.ANY)
    dma = pltpu.SemaphoreType.DMA
    served = pl.pallas_call(
        functools.partial(exchange_kernel, dist, groups, rows),
        out_shape=jax.ShapeDtypeStruct((slots, rows, height, width), base.dtype),
        in_specs=[anywhere] * 4,
        out_specs=pl.BlockSpec(memory_space=pltpu.VMEM),
        scratch_shapes=[
            pltpu.VMEM((slots, rows, rank, model), left.dtype),
            pltpu.VMEM(right.shape, right.dtype),
            pltpu.SMEM((slots, slots), scale.dtype),
            dma((slots, rows)), dma((slots, rows)),
            dma((slots, 2)), dma((slots, 2)),
            dma((slots, rows)), dma((slots, rows)),
            dma((slots, 2)), dma((slots, 2)),
            pltpu.SemaphoreType.REGULAR,
        ],
        compiler_params=pltpu.CompilerParams(collective_id=first, has_side_effects=True, vmem_limit_bytes=VMEM_LIMIT),
        name=f"exchange_{first}",
    )(base, left, right, scale)
    return copy_out(served.reshape(slots, rows * height, width))


def copy_out_kernel(chunks, x, y, sem):
    size = x.shape[1] // chunks
    copies = []
    for j in range(x.shape[0]):
        for i in range(chunks):
            here = pl.ds(i * size, size)
            copies.append(pltpu.make_async_copy(x.at[j, here], y.at[j, here], sem.at[j, i]))
    for copy in copies:
        copy.start()
    for copy in copies:
        copy.wait()


def copy_out(x, chunks=7):
    return pl.pallas_call(
        functools.partial(copy_out_kernel, chunks),
        out_shape=pltpu.HBM(x.shape, x.dtype),
        in_specs=[pl.BlockSpec(memory_space=pltpu.VMEM)],
        out_specs=pl.BlockSpec(memory_space=pl.ANY),
        scratch_shapes=[pltpu.SemaphoreType.DMA((x.shape[0], chunks))],
        compiler_params=pltpu.CompilerParams(vmem_limit_bytes=VMEM_LIMIT),
        name="copy_out",
    )(x)


def local(groups, rows, base, left_factors, right_factors, expert_adapter_scale, placement):
    first = jnp.mod(placement[0] - lax.axis_index("expert"), groups)
    left = jnp.swapaxes(left_factors, 1, 2)
    served = lax.switch(
        first,
        [functools.partial(exchange, o, groups, rows) for o in range(groups)],
        base, left, right_factors, expert_adapter_scale,
    )
    return served


def solution(mesh):
    placed = (
        P("expert", "row", None),
        P("expert", None, "row"),
        P("expert", None, "row"),
        P("expert"),
        P("expert"),
    )
    return jax.shard_map(
        functools.partial(local, mesh.shape["expert"], mesh.shape["row"]),
        mesh=mesh, in_specs=placed, out_specs=P("expert", None, "row"), check_vma=False,
    )
```

time: 180 us -> 178 us (0.989)
  no operation moved by 1% of the time
where the time goes in v2:
time: 178 us
  Pallas kernels  178 us (100%)
    pallas_call x1, Pallas kernels, exchange(): pl.pallas_call(functools.partial(exchange_kernel, dist, groups, rows), ou...  175 us

profile of v2, /device:TPU:16, one launch (start us, length us, event | category | flops | bytes accessed | tf_op | source)
XLA Modules:
  0.0 178.4 jit_solution(8789596374249884848)
XLA Ops:
  0.7 177.7 %conditional.1 = (bf16[2,7168,256]{2,1,0:T(8,128)(2,1)}) conditional(s32[]{:T(128)} %clamp.3, (bf16[2,896,2048]{2,1,0:T(8,128)(2,1)}, bf16[2,8,7168]{2,1,0:T(8,128)(2,1)}, bf16[2,64,256]{2,1,0:T(8,128)(2,1)}, f32[2]{0:T(128)}) %tuple.26, (bf16[2,896,2048]{2,1,0:T(8,128)(2,1)}, bf16[2,8,7168]{2,1,0:T(8,128)(2,1)}, ...), branch_computations={%region_0.1_spmd, %region_1.2_spmd, %region_2.3_spmd, %region_3.4_... | conditional | bytes 8 | solution.py:243
  0.7 174.6 %exchange_2.1 = bf16[2,8,896,256]{3,2,1,0:T(8,128)(2,1)S(1)} custom-call(bf16[2,896,2048]{2,1,0:T(8,128)(2,1)} %get-tuple-element.73.base, bf16[2,8,7168]{2,1,0:T(8,128)(2,1)} %get-tuple-element.51.left, bf16[2,64,256]{2,1,0:T(8,128)(2,1)} %get-tuple-element.77.right, f32[2]{0:T(128)} %get-tuple-element.81.scale), custom_call_target="tpu_custom_call" | custom-call | tf_op jit(solution)/shard_map/cond/branch_2_fun/exchange_2/pallas_call | solution.py:194
  175.3 3.1 %copy_out.6 = bf16[2,7168,256]{2,1,0:T(8,128)(2,1)} custom-call(bf16[2,7168,256]{2,1,0:T(8,128)(2,1)S(1)} %bitcast.9), custom_call_target="tpu_custom_call" | custom-call | tf_op jit(solution)/shard_map/cond/branch_2_fun/copy_out/pallas_call | solution.py:229

commit v3 on v2

--- a/solution.py
+++ b/solution.py
@@ -8,7 +8,6 @@
 from jax.sharding import PartitionSpec as P
 
 MESH = pl.DeviceIdType.MESH
-WINDOW = 12
 LANES = 128
 VMEM_LIMIT = 24 << 20
 
@@ -17,17 +16,14 @@
     return next(u for u in (1, 2, 4, 8) if u * height % LANES == 0)
 
 
-def near_turn(q, half):
-    quarter = half // 2
-    return (q + q // quarter) % half + quarter * (1 - (q + half - 1) // half)
-
-
 def piece_order(rows, slots, lead):
-    half = rows // 2
+    half, quarter = rows // 2, rows // 4
+    far = [*range(half, half + quarter), *reversed(range(half + quarter, rows))]
+    near = [m for pair in zip(range(quarter, half), [*range(1, quarter), 0]) for m in pair]
+    turns = [(lead + i) % slots for i in range(slots)]
     order = []
     for q in range(half):
-        for m in (half + q, near_turn(q, half)):
-            order += [(m, (lead + i) % slots) for i in range(slots)]
+        order += [(far[q], j) for j in turns] + [(near[q], j) for j in turns]
     return order
 
 
@@ -66,31 +62,47 @@
 
     cuts = [(0, height)]
     if height % LANES == 0 and height > LANES:
-        top = (height // LANES + 1) // 2 * LANES
+        top = max(1, 3 * height // LANES // 4) * LANES
         cuts = [(0, top), (top, height - top)]
 
-    def tail(j, i):
+    def cut(i):
+        if len(cuts) == 1:
+            return piece(mirror, lead)
         off, size = cuts[i]
-        c = r ^ (rows - 1)
-        src = base.at[j, pl.ds(off, size), pl.ds(pl.multiple_of(c * width, width), width)]
-        return remote(src, got.at[j, r, pl.ds(off, size)], tsend.at[j, i], trecv.at[j, i], c, to[j])
+        c = r ^ mirror
+        src = base.at[lead, pl.ds(off, size), pl.ds(pl.multiple_of(c * width, width), width)]
+        return remote(src, got.at[lead, r, pl.ds(off, size)], tsend.at[i], trecv.at[i], c, to[lead])
 
     def piece(m, j):
-        if m == rows - 1 and len(cuts) > 1:
-            return [tail(j, i) for i in range(len(cuts))]
-        if j == lead and m in (half, mirror):
-            m = jnp.where(inner, half + mirror - m, m)
         c = r ^ m
         src = base.at[j, :, pl.ds(pl.multiple_of(c * width, width), width)]
         if dist[j] == 0 and isinstance(m, int) and m == 0:
-            return [pltpu.make_async_copy(src, got.at[j, r], recv.at[j, 0])]
-        return [remote(src, got.at[j, r], send.at[j, m], recv.at[j, m], c, to[j])]
-
-    pending = piece(*order[0])
+            return pltpu.make_async_copy(src, got.at[j, r], recv.at[j, 0])
+        return remote(src, got.at[j, r], send.at[j, m], recv.at[j, m], c, to[j])
+
+    leads = [m for m, j in order if j == lead and m >= half]
+
+    def send_piece(m, j):
+        if j != lead or m < half:
+            piece(m, j).start()
+            return
+        q = leads.index(m)
+
+        @pl.when(inner)
+        def _():
+            piece(leads[q - 1], j).start()
+
+        @pl.when(jnp.logical_not(inner))
+        def _():
+            if m == mirror:
+                for i in range(len(cuts)):
+                    cut(i).start()
+            else:
+                piece(m, j).start()
 
     @pl.when(inner)
     def _():
-        pending[0].start()
+        cut(0).start()
         pl.semaphore_wait(go, 1)
 
     @pl.when(jnp.logical_not(inner))
@@ -114,7 +126,7 @@
         copy.start()
         first.append(copy)
 
-    pl.when(jnp.logical_not(inner))(pending[0].start)
+    pl.when(jnp.logical_not(inner))(piece(*order[0]).start)
 
     def left_round(mask, held):
         copies = []
@@ -140,13 +152,9 @@
             for copy in waiting:
                 copy.wait()
             waiting = left_round(*rounds[at[k]])
-        if len(pending) >= WINDOW:
-            pending.pop(0).wait_send()
-        copies = piece(m, j)
-        for copy in copies:
-            copy.start()
-        if not (m == 0 and dist[j] == 0):
-            pending += copies
+        send_piece(m, j)
+    for i in range(1, len(cuts)):
+        pl.when(inner)(cut(i).start)
     for copy in waiting:
         copy.wait()
 
@@ -158,8 +166,12 @@
         a = left_all[j, :, :, columns].reshape(rank_all, size)
         return lax.dot_general(a, right_got[j], (((0,), (0,)), ((), ())), preferred_element_type=jnp.float32)
 
+    blocks = rows // unit
+    calm = blocks - blocks // 4
+
     def turn(t, carry):
-        m, j = t // slots * unit, t % slots
+        q, j = t // slots, lax.rem(lead + 1 + t, slots)
+        m = jnp.where(q < calm, q, calm + blocks - 1 - q) * unit
         row = (r ^ m) // unit * unit
         for u in range(unit):
             block = got.at[j, r ^ (m + u)]
@@ -170,18 +182,19 @@
             got[j, row + u] = (got[j, row + u].astype(jnp.float32) + scale_got[j, j] * part).astype(got.dtype)
         return carry
 
-    last = 1 if len(cuts) > 1 else 0
-    lax.fori_loop(0, rows * slots // unit - last * slots, turn, 0)
-
-    row = r ^ (rows - 1)
-    for j in range(slots if last else 0):
-        for i, (off, size) in enumerate(cuts):
-            tail(j, i).wait_recv()
-            here = pl.ds(off, size)
-            part = scale_got[j, j] * merge(j, row, off, size)
-            got[j, row, here] = (got[j, row, here].astype(jnp.float32) + part).astype(got.dtype)
-    for copy in pending:
-        copy.wait_send()
+    lax.fori_loop(0, blocks * slots - (len(cuts) > 1), turn, 0)
+    row = r ^ mirror
+    for i, (off, size) in enumerate(cuts if len(cuts) > 1 else ()):
+        cut(i).wait_recv()
+        here = pl.ds(off, size)
+        part = scale_got[lead, lead] * merge(lead, row, off, size)
+        got[lead, row, here] = (got[lead, row, here].astype(jnp.float32) + part).astype(got.dtype)
+    for m, j in order:
+        if (m, j) == (mirror, lead):
+            for i in range(len(cuts)):
+                cut(i).wait_send()
+        elif m or dist[j]:
+            piece(m, j).wait_send()
 
 
 def exchange(first, groups, rows, base, left, right, scale):
@@ -201,7 +214,7 @@
             pltpu.VMEM(right.shape, right.dtype),
             pltpu.SMEM((slots, slots), scale.dtype),
             dma((slots, rows)), dma((slots, rows)),
-            dma((slots, 2)), dma((slots, 2)),
+            dma((2,)), dma((2,)),
             dma((slots, rows)), dma((slots, rows)),
             dma((slots, 2)), dma((slots, 2)),
             pltpu.SemaphoreType.REGULAR,

time: 178 us -> 176 us (0.989)
  Pallas kernels: 178 us -> 175 us
    pallas_call x1, Pallas kernels: 175 us -> 172 us  [exchange(): pl.pallas_call(functools.partial(exchange_kernel, dist, groups, rows), ou...]
where the time goes in v3:
time: 176 us
  Pallas kernels  175 us (99%)
    pallas_call x1, Pallas kernels, exchange(): pl.pallas_call(functools.partial(exchange_kernel, dist, groups, rows), ou...  172 us

profile of v3, /device:TPU:16, one launch (start us, length us, event | category | flops | bytes accessed | tf_op | source)
XLA Modules:
  0.0 175.7 jit_solution(13813345401471733849)
XLA Ops:
  0.7 175.0 %conditional.1 = (bf16[2,7168,256]{2,1,0:T(8,128)(2,1)}) conditional(s32[]{:T(128)} %clamp.3, (bf16[2,896,2048]{2,1,0:T(8,128)(2,1)}, bf16[2,8,7168]{2,1,0:T(8,128)(2,1)}, bf16[2,64,256]{2,1,0:T(8,128)(2,1)}, f32[2]{0:T(128)}) %tuple.26, (bf16[2,896,2048]{2,1,0:T(8,128)(2,1)}, bf16[2,8,7168]{2,1,0:T(8,128)(2,1)}, ...), branch_computations={%region_0.1_spmd, %region_1.2_spmd, %region_2.3_spmd, %region_3.4_... | conditional | bytes 8 | solution.py:256
  0.7 171.9 %exchange_0.1 = bf16[2,8,896,256]{3,2,1,0:T(8,128)(2,1)S(1)} custom-call(bf16[2,896,2048]{2,1,0:T(8,128)(2,1)} %get-tuple-element.71.base, bf16[2,8,7168]{2,1,0:T(8,128)(2,1)} %get-tuple-element.42.left, bf16[2,64,256]{2,1,0:T(8,128)(2,1)} %get-tuple-element.75.right, f32[2]{0:T(128)} %get-tuple-element.79.scale), custom_call_target="tpu_custom_call" | custom-call | tf_op jit(solution)/shard_map/cond/branch_0_fun/exchange_0/pallas_call | solution.py:207
  172.6 3.1 %copy_out.4 = bf16[2,7168,256]{2,1,0:T(8,128)(2,1)} custom-call(bf16[2,7168,256]{2,1,0:T(8,128)(2,1)S(1)} %bitcast.7), custom_call_target="tpu_custom_call" | custom-call | tf_op jit(solution)/shard_map/cond/branch_0_fun/copy_out/pallas_call | solution.py:242

commit v4 on v3

--- a/solution.py
+++ b/solution.py
@@ -16,25 +16,24 @@
     return next(u for u in (1, 2, 4, 8) if u * height % LANES == 0)
 
 
-def piece_order(rows, slots, lead):
+def piece_order(rows):
     half, quarter = rows // 2, rows // 4
     far = [*range(half, half + quarter), *reversed(range(half + quarter, rows))]
     near = [m for pair in zip(range(quarter, half), [*range(1, quarter), 0]) for m in pair]
-    turns = [(lead + i) % slots for i in range(slots)]
-    order = []
-    for q in range(half):
-        order += [(far[q], j) for j in turns] + [(near[q], j) for j in turns]
-    return order
+    return [m for pair in zip(far, near) for m in pair]
 
 
 def exchange_kernel(dist, groups, rows, base, left, right, scale, got, left_all, right_got, scale_got,
-                    send, recv, tsend, trecv, lsend, lrecv, ssend, srecv, go):
+                    held, left_own, right_all, scale_own,
+                    send, recv, tsend, trecv, lsend, lrecv, ssend, srecv, go,
+                    asend, arecv, rsend, rrecv, near):
     r, g = lax.axis_index("row"), lax.axis_index("expert")
     slots, _, height, width = got.shape
     half, quarter = rows // 2, rows // 4
     to = [lax.rem(g + d, groups) for d in dist]
     lead = min(range(slots), key=lambda j: min(dist[j], groups - dist[j]))
-    order = piece_order(rows, slots, lead)
+    other = 1 - lead
+    order = piece_order(rows)
     mirror = half + quarter
     inner = jnp.logical_and(r >= quarter, r < rows - quarter)
 
@@ -75,22 +74,23 @@
 
     def piece(m, j):
         c = r ^ m
-        src = base.at[j, :, pl.ds(pl.multiple_of(c * width, width), width)]
+        columns = pl.ds(pl.multiple_of(c * width, width), width)
+        src = base.at[j, :, columns] if j == lead else held.at[:, columns]
         if dist[j] == 0 and isinstance(m, int) and m == 0:
             return pltpu.make_async_copy(src, got.at[j, r], recv.at[j, 0])
         return remote(src, got.at[j, r], send.at[j, m], recv.at[j, m], c, to[j])
 
-    leads = [m for m, j in order if j == lead and m >= half]
-
-    def send_piece(m, j):
-        if j != lead or m < half:
-            piece(m, j).start()
+    leads = [m for m in order if m >= half]
+
+    def send_lead(m):
+        if m < half:
+            piece(m, lead).start()
             return
         q = leads.index(m)
 
         @pl.when(inner)
         def _():
-            piece(leads[q - 1], j).start()
+            piece(leads[q - 1], lead).start()
 
         @pl.when(jnp.logical_not(inner))
         def _():
@@ -98,7 +98,19 @@
                 for i in range(len(cuts)):
                     cut(i).start()
             else:
-                piece(m, j).start()
+                piece(m, lead).start()
+
+    unit = unit_of(height)
+    span = unit * height
+    loads = [
+        pltpu.make_async_copy(base.at[other], held, near.at[0]),
+        pltpu.make_async_copy(right.at[other], right_all.at[r], near.at[1]),
+        pltpu.make_async_copy(left.at[other, :, pl.ds(pl.multiple_of(r // unit * span, LANES), span)],
+                              left_own.at[r], near.at[2]),
+        pltpu.make_async_copy(scale, scale_own, near.at[3]),
+    ]
+    for copy in loads:
+        copy.start()
 
     @pl.when(inner)
     def _():
@@ -110,91 +122,128 @@
         pl.semaphore_signal(go, inc=1, device_id={"row": r ^ quarter, "expert": g}, device_id_type=MESH)
 
     first = []
-    for j in range(slots):
-        for src, dst, s, t in (
-            (left.at[j], left_all.at[j, r], lsend.at[j, 0], lrecv.at[j, 0]),
-            (right.at[j], right_got.at[j], ssend.at[j, 0], srecv.at[j, 0]),
-            (scale, scale_got.at[j], ssend.at[j, 1], srecv.at[j, 1]),
-        ):
-            if dist[j] == 0:
-                copy = pltpu.make_async_copy(src, dst, t)
-            else:
-                copy = remote(src, dst, s, t, r, to[j])
+    for src, dst, s, t in (
+        (left.at[lead], left_all.at[r], lsend.at[0], lrecv.at[0]),
+        (right.at[lead], right_got, ssend.at[0], srecv.at[0]),
+        (scale, scale_got, ssend.at[1], srecv.at[1]),
+    ):
+        if dist[lead] == 0:
+            copy = pltpu.make_async_copy(src, dst, t)
+        else:
+            copy = remote(src, dst, s, t, r, to[lead])
+        first.append(copy)
+    first.append(remote(left.at[lead], left_all.at[r], lsend.at[half], lrecv.at[half], r ^ half, to[lead]))
+    for m in (*range(half, rows), *range(1, half)):
+        c = r ^ m
+        part = left.at[other, :, pl.ds(pl.multiple_of(c // unit * span, LANES), span)]
+        first.append(remote(part, left_own.at[r], asend.at[m], arecv.at[m], c, g))
+    for m in (half, *range(1, half)):
+        first.append(remote(right.at[other], right_all.at[r], rsend.at[0, m], rrecv.at[0, m], r ^ m, g))
+    for copy in first:
+        copy.start()
+
+    pl.when(jnp.logical_not(inner))(piece(order[0], lead).start)
+
+    def right_round():
+        part = right_all.at[r ^ half]
+        copies = [remote(part, part, rsend.at[1, m], rrecv.at[1, m], r ^ m, g) for m in range(1, half)]
+        for copy in copies:
             copy.start()
-            first.append(copy)
-        copy = remote(left.at[j], left_all.at[j, r], lsend.at[j, half], lrecv.at[j, half], r ^ half, to[j])
-        copy.start()
-        first.append(copy)
-
-    pl.when(jnp.logical_not(inner))(piece(*order[0]).start)
-
-    def left_round(mask, held):
+        return copies
+
+    def left_round(mask, have):
         copies = []
-        for s in held:
-            for j in range(slots):
-                part = left_all.at[j, r ^ s]
-                copy = remote(part, part, lsend.at[j, mask | s], lrecv.at[j, mask | s], r ^ mask, g)
-                copy.start()
-                copies.append(copy)
+        for s in have:
+            part = left_all.at[r ^ s]
+            copy = remote(part, part, lsend.at[mask | s], lrecv.at[mask | s], r ^ mask, g)
+            copy.start()
+            copies.append(copy)
         return copies
 
     rounds = []
-    mask, held = half // 2, [0, half]
+    mask, have = half // 2, [0, half]
     while mask:
-        rounds.append((mask, list(held)))
-        held += [s | mask for s in held]
+        rounds.append((mask, list(have)))
+        have += [s | mask for s in have]
         mask //= 2
 
-    at = {(2 + i) * len(order) // 4: i for i in range(len(rounds))}
-    waiting = first
-    for k, (m, j) in enumerate(order[1:], 1):
-        if k in at:
-            for copy in waiting:
-                copy.wait()
-            waiting = left_round(*rounds[at[k]])
-        send_piece(m, j)
+    early = len(order) if dist[lead] == 0 else len(order) // 4
+    for m in order[1:early]:
+        send_lead(m)
+    ahead = [first[3], first[3 + rows]]
+    first[0].wait()
+    for copy in ahead:
+        copy.wait_recv()
+    waiting = right_round() + left_round(*rounds[0])
+    for m in order[early:]:
+        send_lead(m)
+    for copy in ahead:
+        copy.wait_send()
+    for copy in first[1:3] + first[4:3 + rows] + first[4 + rows:] + waiting + loads:
+        copy.wait()
+    waiting = left_round(*rounds[1])
+
+    def expand(lhs, rhs):
+        return lax.dot_general(lhs, rhs, (((0,), (0,)), ((), ())), preferred_element_type=jnp.float32)
+
+    rank_all = left_all.shape[0] * left_all.shape[1]
+
+    def merge_held(q, carry):
+        c = r ^ q ^ half
+        delta = expand(left_own[...].reshape(rank_all, span), right_all[c])
+        part = delta[:height]
+        for u in range(1, unit):
+            part = jnp.where(lax.rem(r, unit) == u, delta[u * height:(u + 1) * height], part)
+        here = pl.ds(pl.multiple_of(c * width, width), width)
+        held[:, here] = (held[:, here].astype(jnp.float32) + scale_own[other] * part).astype(held.dtype)
+        return carry
+
+    lax.fori_loop(0, rows, merge_held, 0)
+    for m in order:
+        piece(m, other).start()
     for i in range(1, len(cuts)):
         pl.when(inner)(cut(i).start)
     for copy in waiting:
         copy.wait()
-
-    unit = unit_of(height)
-    rank_all = left_all.shape[1] * left_all.shape[2]
-
-    def merge(j, row, off, size):
+    for i in range(2, len(rounds)):
+        for copy in left_round(*rounds[i]):
+            copy.wait()
+
+    def merge(row, off, size):
         columns = pl.ds(pl.multiple_of(row * height + off, LANES), size)
-        a = left_all[j, :, :, columns].reshape(rank_all, size)
-        return lax.dot_general(a, right_got[j], (((0,), (0,)), ((), ())), preferred_element_type=jnp.float32)
+        return expand(left_all[:, :, columns].reshape(rank_all, size), right_got[...])
 
     blocks = rows // unit
     calm = blocks - blocks // 4
 
-    def turn(t, carry):
-        q, j = t // slots, lax.rem(lead + 1 + t, slots)
+    def turn(q, carry):
         m = jnp.where(q < calm, q, calm + blocks - 1 - q) * unit
         row = (r ^ m) // unit * unit
         for u in range(unit):
-            block = got.at[j, r ^ (m + u)]
-            remote(block, block, send.at[j, m + u], recv.at[j, m + u], r ^ 1, g).wait_recv()
-        delta = merge(j, row, 0, unit * height)
+            block = got.at[lead, r ^ (m + u)]
+            remote(block, block, send.at[lead, m + u], recv.at[lead, m + u], r ^ 1, g).wait_recv()
+        delta = merge(row, 0, span)
         for u in range(unit):
             part = delta[u * height:(u + 1) * height]
-            got[j, row + u] = (got[j, row + u].astype(jnp.float32) + scale_got[j, j] * part).astype(got.dtype)
+            got[lead, row + u] = (got[lead, row + u].astype(jnp.float32) + scale_got[lead] * part).astype(got.dtype)
         return carry
 
-    lax.fori_loop(0, blocks * slots - (len(cuts) > 1), turn, 0)
+    lax.fori_loop(0, blocks - (len(cuts) > 1), turn, 0)
+    for m in order:
+        piece(m, other).wait_recv()
     row = r ^ mirror
     for i, (off, size) in enumerate(cuts if len(cuts) > 1 else ()):
         cut(i).wait_recv()
         here = pl.ds(off, size)
-        part = scale_got[lead, lead] * merge(lead, row, off, size)
+        part = scale_got[lead] * merge(row, off, size)
         got[lead, row, here] = (got[lead, row, here].astype(jnp.float32) + part).astype(got.dtype)
-    for m, j in order:
-        if (m, j) == (mirror, lead):
+    for m in order:
+        piece(m, other).wait_send()
+        if m == mirror:
             for i in range(len(cuts)):
                 cut(i).wait_send()
-        elif m or dist[j]:
-            piece(m, j).wait_send()
+        elif m or dist[lead]:
+            piece(m, lead).wait_send()
 
 
 def exchange(first, groups, rows, base, left, right, scale):
@@ -210,14 +259,21 @@
         in_specs=[anywhere] * 4,
         out_specs=pl.BlockSpec(memory_space=pltpu.VMEM),
         scratch_shapes=[
-            pltpu.VMEM((slots, rows, rank, model), left.dtype),
-            pltpu.VMEM(right.shape, right.dtype),
-            pltpu.SMEM((slots, slots), scale.dtype),
+            pltpu.VMEM((rows, rank, model), left.dtype),
+            pltpu.VMEM(right.shape[1:], right.dtype),
+            pltpu.SMEM(scale.shape, scale.dtype),
+            pltpu.VMEM((height, total), base.dtype),
+            pltpu.VMEM((rows, rank, unit_of(height) * height), left.dtype),
+            pltpu.VMEM((rows, *right.shape[1:]), right.dtype),
+            pltpu.SMEM(scale.shape, scale.dtype),
             dma((slots, rows)), dma((slots, rows)),
             dma((2,)), dma((2,)),
-            dma((slots, rows)), dma((slots, rows)),
-            dma((slots, 2)), dma((slots, 2)),
+            dma((rows,)), dma((rows,)),
+            dma((2,)), dma((2,)),
             pltpu.SemaphoreType.REGULAR,
+            dma((rows,)), dma((rows,)),
+            dma((2, rows)), dma((2, rows)),
+            dma((4,)),
         ],
         compiler_params=pltpu.CompilerParams(collective_id=first, has_side_effects=True, vmem_limit_bytes=VMEM_LIMIT),
         name=f"exchange_{first}",

time: 176 us -> 176 us (level)
  no operation moved by 1% of the time
where the time goes in v4:
time: 176 us
  Pallas kernels  175 us (99%)
    pallas_call x1, Pallas kernels, exchange(): pl.pallas_call(functools.partial(exchange_kernel, dist, groups, rows), ou...  172 us

profile of v4, /device:TPU:16, one launch (start us, length us, event | category | flops | bytes accessed | tf_op | source)
XLA Modules:
  0.0 175.8 jit_solution(14899940077184708481)
XLA Ops:
  0.7 175.1 %conditional.1 = (bf16[2,7168,256]{2,1,0:T(8,128)(2,1)}) conditional(s32[]{:T(128)} %clamp.3, (bf16[2,896,2048]{2,1,0:T(8,128)(2,1)}, bf16[2,8,7168]{2,1,0:T(8,128)(2,1)}, bf16[2,64,256]{2,1,0:T(8,128)(2,1)}, f32[2]{0:T(128)}) %tuple.26, (bf16[2,896,2048]{2,1,0:T(8,128)(2,1)}, bf16[2,8,7168]{2,1,0:T(8,128)(2,1)}, ...), branch_computations={%region_0.1_spmd, %region_1.2_spmd, %region_2.3_spmd, %region_3.4_... | conditional | bytes 8 | solution.py:312
  0.7 172.0 %exchange_1.1 = bf16[2,8,896,256]{3,2,1,0:T(8,128)(2,1)S(1)} custom-call(bf16[2,896,2048]{2,1,0:T(8,128)(2,1)} %get-tuple-element.72.base, bf16[2,8,7168]{2,1,0:T(8,128)(2,1)} %get-tuple-element.47.left, bf16[2,64,256]{2,1,0:T(8,128)(2,1)} %get-tuple-element.76.right, f32[2]{0:T(128)} %get-tuple-element.80.scale), custom_call_target="tpu_custom_call" | custom-call | tf_op jit(solution)/shard_map/cond/branch_1_fun/exchange_1/pallas_call | solution.py:256
  172.7 3.1 %copy_out.5 = bf16[2,7168,256]{2,1,0:T(8,128)(2,1)} custom-call(bf16[2,7168,256]{2,1,0:T(8,128)(2,1)S(1)} %bitcast.8), custom_call_target="tpu_custom_call" | custom-call | tf_op jit(solution)/shard_map/cond/branch_1_fun/copy_out/pallas_call | solution.py:298

commit v5 on v4

--- a/solution.py
+++ b/solution.py
@@ -199,7 +199,7 @@
         return carry
 
     lax.fori_loop(0, rows, merge_held, 0)
-    for m in order:
+    for m in order[::2] + order[1::2] if dist[lead] == 0 else order:
         piece(m, other).start()
     for i in range(1, len(cuts)):
         pl.when(inner)(cut(i).start)

time: 176 us -> 174 us (0.989)
  no operation moved by 1% of the time
where the time goes in v5:
time: 174 us
  Pallas kernels  174 us (100%)
    pallas_call x1, Pallas kernels, exchange(): pl.pallas_call(functools.partial(exchange_kernel, dist, groups, rows), ou...  170 us

profile of v5, /device:TPU:16, one launch (start us, length us, event | category | flops | bytes accessed | tf_op | source)
XLA Modules:
  0.0 174.3 jit_solution(11836042695996460577)
XLA Ops:
  0.7 173.6 %conditional.1 = (bf16[2,7168,256]{2,1,0:T(8,128)(2,1)}) conditional(s32[]{:T(128)} %clamp.3, (bf16[2,896,2048]{2,1,0:T(8,128)(2,1)}, bf16[2,8,7168]{2,1,0:T(8,128)(2,1)}, bf16[2,64,256]{2,1,0:T(8,128)(2,1)}, f32[2]{0:T(128)}) %tuple.26, (bf16[2,896,2048]{2,1,0:T(8,128)(2,1)}, bf16[2,8,7168]{2,1,0:T(8,128)(2,1)}, ...), branch_computations={%region_0.1_spmd, %region_1.2_spmd, %region_2.3_spmd, %region_3.4_... | conditional | bytes 8 | solution.py:312
  0.7 170.5 %exchange_3.1 = bf16[2,8,896,256]{3,2,1,0:T(8,128)(2,1)S(1)} custom-call(bf16[2,896,2048]{2,1,0:T(8,128)(2,1)} %get-tuple-element.74.base, bf16[2,8,7168]{2,1,0:T(8,128)(2,1)} %get-tuple-element.55.left, bf16[2,64,256]{2,1,0:T(8,128)(2,1)} %get-tuple-element.78.right, f32[2]{0:T(128)} %get-tuple-element.82.scale), custom_call_target="tpu_custom_call" | custom-call | tf_op jit(solution)/shard_map/cond/branch_3_fun/exchange_3/pallas_call | solution.py:256
  171.2 3.1 %copy_out.7 = bf16[2,7168,256]{2,1,0:T(8,128)(2,1)} custom-call(bf16[2,7168,256]{2,1,0:T(8,128)(2,1)S(1)} %bitcast.10), custom_call_target="tpu_custom_call" | custom-call | tf_op jit(solution)/shard_map/cond/branch_3_fun/copy_out/pallas_call | solution.py:298

commit v6 on v5

--- a/solution.py
+++ b/solution.py
@@ -199,8 +199,11 @@
         return carry
 
     lax.fori_loop(0, rows, merge_held, 0)
-    for m in order[::2] + order[1::2] if dist[lead] == 0 else order:
-        piece(m, other).start()
+    far, close = order[::2], order[1::2]
+    bunch = len(far) if dist[lead] == 0 else len(far) // 2
+    for i in range(0, len(far), bunch):
+        for m in far[i:i + bunch] + close[i:i + bunch]:
+            piece(m, other).start()
     for i in range(1, len(cuts)):
         pl.when(inner)(cut(i).start)
     for copy in waiting:

time: 174 us -> 176 us (1.011)
  no operation moved by 1% of the time
where the time goes in v6:
time: 176 us
  Pallas kernels  175 us (99%)
    pallas_call x1, Pallas kernels, exchange(): pl.pallas_call(functools.partial(exchange_kernel, dist, groups, rows), ou...  172 us

profile of v6, /device:TPU:16, one launch (start us, length us, event | category | flops | bytes accessed | tf_op | source)
XLA Modules:
  0.0 175.8 jit_solution(16731841919901897006)
XLA Ops:
  0.7 175.1 %conditional.1 = (bf16[2,7168,256]{2,1,0:T(8,128)(2,1)}) conditional(s32[]{:T(128)} %clamp.3, (bf16[2,896,2048]{2,1,0:T(8,128)(2,1)}, bf16[2,8,7168]{2,1,0:T(8,128)(2,1)}, bf16[2,64,256]{2,1,0:T(8,128)(2,1)}, f32[2]{0:T(128)}) %tuple.26, (bf16[2,896,2048]{2,1,0:T(8,128)(2,1)}, bf16[2,8,7168]{2,1,0:T(8,128)(2,1)}, ...), branch_computations={%region_0.1_spmd, %region_1.2_spmd, %region_2.3_spmd, %region_3.4_... | conditional | bytes 8 | solution.py:315
  0.7 172.0 %exchange_1.1 = bf16[2,8,896,256]{3,2,1,0:T(8,128)(2,1)S(1)} custom-call(bf16[2,896,2048]{2,1,0:T(8,128)(2,1)} %get-tuple-element.72.base, bf16[2,8,7168]{2,1,0:T(8,128)(2,1)} %get-tuple-element.47.left, bf16[2,64,256]{2,1,0:T(8,128)(2,1)} %get-tuple-element.76.right, f32[2]{0:T(128)} %get-tuple-element.80.scale), custom_call_target="tpu_custom_call" | custom-call | tf_op jit(solution)/shard_map/cond/branch_1_fun/exchange_1/pallas_call | solution.py:259
  172.7 3.1 %copy_out.5 = bf16[2,7168,256]{2,1,0:T(8,128)(2,1)} custom-call(bf16[2,7168,256]{2,1,0:T(8,128)(2,1)S(1)} %bitcast.8), custom_call_target="tpu_custom_call" | custom-call | tf_op jit(solution)/shard_map/cond/branch_1_fun/copy_out/pallas_call | solution.py:301
